TPU v7x, 32 devices: a whole 2x2x4 slice. The times are simulated.
32 devices in a mesh: vox: 8 (over z, core), sta: 4 (over y, x).
Axes of the slice: x: 2, y: 2, z: 4, core: 2. Of those that a mesh axis runs over, the one named last changes fastest.
Arguments:
- green_tensor: bfloat16 [4, 6, 256, 1024], P('sta', None, None, 'vox'), may hold values from -0.078125 to 0.078125
- strain: bfloat16 [8, 6, 256, 1024], P('sta', None, None, 'vox'), may hold values from -6 to 6
- pair_events: int32 [4, 8], P('sta'), may hold values from -1 to 7, as said below
- pair_counts: int32 [4], P('sta'), may hold values from 6 to 8, as said below
- residuals: float32 [4, 8, 256], P('sta'), may hold values from -0.375 to 0.375
Outputs:
- kernel: float32 [1024], P(('vox', 'sta'))
Inputs may be any that keep to these rules, and one draw needn't show every extreme that they name: `pair_events`: within a station the live entries are distinct earthquakes; slots at or beyond the station's count hold -1. `pair_counts`: some station has exactly 8 live slots in every draw.
All inputs are finite; a program needn't handle non-finite values.
Results may differ from a plain program's by a relative error of at most 0.0029.
Values may be sent and summed in bfloat16 or wider, within the bound.
A program may use at most 64 MiB of HBM per device.

v0:
```python
import functools

import jax
import jax.numpy as jnp
from jax import lax
from jax.experimental import pallas as pl
from jax.experimental.pallas import tpu as pltpu
from jax.sharding import PartitionSpec as P

LANES = 128
F32 = jnp.float32
BF16 = jnp.bfloat16


def kernel(
    n, events_ref, counts_ref, resid_ref, green_hbm, strain_hbm, out_ref,
    green, strain, packed_green, packed_strain, all_comb, all_green, all_strain, adjoint,
    load_sem, send_sem, recv_sem,
):
    me = lax.axis_index("sta")
    comps, nt, vox = green.shape
    local_events = strain.shape[0]
    slots = resid_ref.shape[0]
    width = vox // n
    per_tile = LANES // width
    full = comps // per_tile
    rest = comps % per_tile
    fit = min(per_tile // rest, local_events) if rest else 1
    blocks = nt // LANES

    def peer(d):
        pair = lax.rem(me // 2 + d // 2, n // 2)
        return 2 * pair + lax.rem(me + d, 2)

    order = list(range(n - 1, 0, -1))
    load_green = pltpu.make_async_copy(green_hbm.at[0], green, load_sem.at[0])
    load_strain = pltpu.make_async_copy(strain_hbm, strain, load_sem.at[1])
    load_green.start()
    load_strain.start()

    barrier = pltpu.get_barrier_semaphore()
    for d in order:
        pl.semaphore_signal(
            barrier, inc=1, device_id={"sta": peer(d)}, device_id_type=pl.DeviceIdType.MESH
        )

    def send(kind, src, dst, d):
        copy = pltpu.make_async_remote_copy(
            src_ref=src,
            dst_ref=dst.at[me],
            send_sem=send_sem.at[kind, d],
            recv_sem=recv_sem.at[kind, me],
            device_id={"sta": peer(d)},
            device_id_type=pl.DeviceIdType.MESH,
        )
        copy.start()
        return copy

    def wait_from(kind, dst, j):
        pltpu.make_async_remote_copy(
            src_ref=dst.at[j],
            dst_ref=dst.at[j],
            send_sem=send_sem.at[kind, 0],
            recv_sem=recv_sem.at[kind, j],
            device_id={"sta": j},
            device_id_type=pl.DeviceIdType.MESH,
        ).wait_recv()

    rows = lax.broadcasted_iota(jnp.int32, (all_comb.shape[1], nt), 0)
    comb = jnp.zeros((all_comb.shape[1], nt), F32)
    for p in range(slots):
        event = jnp.where(p < counts_ref[0], events_ref[0, p], -1)
        comb = comb + jnp.where(rows == event, resid_ref[p : p + 1, :], 0.0)
    all_comb[me] = comb

    lane = lax.broadcasted_iota(jnp.int32, (LANES, LANES), 0)
    column = lax.broadcasted_iota(jnp.int32, (LANES, LANES), 1)

    def pick(j, slot):
        inside = (column >= slot * width) & (column < (slot + 1) * width)
        return inside & (lane == column + (j - slot) * width)

    def as_matrix(masks):
        return jnp.concatenate([jnp.where(m, 1.0, 0.0).astype(BF16) for m in masks], axis=0)

    def gathered(tiles, matrix):
        wide = jnp.concatenate(tiles, axis=1)
        return jnp.dot(wide, matrix[: len(tiles) * LANES], preferred_element_type=F32).astype(BF16)

    def pack_green(j, masks, matrix, dst, index):
        for a in range(full):
            dst[index, a] = gathered([green[a * per_tile + k] for k in range(per_tile)], matrix)
        if rest:
            repeated = []
            for k in range(rest):
                hit = masks[k]
                for i in range(1, fit):
                    hit = hit | masks[i * rest + k]
                repeated.append(hit)
            dst[index, full] = gathered(
                [green[full * per_tile + k] for k in range(rest)], as_matrix(repeated)
            )

    def pack_strain(matrix, dst, index):
        tile = 0
        for e in range(local_events):
            for a in range(full):
                dst[index, tile] = gathered(
                    [strain[e, a * per_tile + k] for k in range(per_tile)], matrix
                )
                tile += 1
        if rest:
            for e in range(0, local_events, fit):
                dst[index, tile] = gathered(
                    [strain[e + i, full * per_tile + k] for i in range(fit) for k in range(rest)],
                    matrix,
                )
                tile += 1

    matrices = {}
    for d in order + [0]:
        j = peer(d)
        masks = [pick(j, slot) for slot in range(per_tile)]
        matrices[d] = (j, masks, as_matrix(masks))

    load_green.wait()
    copies = []
    pl.semaphore_wait(barrier, n - 1)
    for d in order:
        copies.append(send(0, all_comb.at[me], all_comb, d))
    waiting = None
    for d in order:
        pack_green(*matrices[d], packed_green, d)
        if waiting is not None:
            copies.append(send(1, packed_green.at[waiting], all_green, waiting))
        waiting = d
    pack_green(*matrices[0], all_green, me)
    copies.append(send(1, packed_green.at[waiting], all_green, waiting))
    load_strain.wait()
    waiting = None
    for d in order:
        pack_strain(matrices[d][2], packed_strain, d)
        if waiting is not None:
            copies.append(send(2, packed_strain.at[waiting], all_strain, waiting))
        waiting = d
    pack_strain(matrices[0][2], all_strain, me)
    copies.append(send(2, packed_strain.at[waiting], all_strain, waiting))

    for d in order:
        wait_from(0, all_comb, peer(d))
    for d in order:
        wait_from(1, all_green, peer(d))

    later = column >= lane
    nothing = jnp.zeros((LANES, LANES), BF16)
    tiles = all_green.shape[1]

    @pl.loop(0, all_comb.shape[1])
    def _(e):
        total = jnp.zeros((nt, tiles * LANES), F32)
        for s in range(n):
            wave = all_comb[s, pl.ds(e, 1), :]
            turned = []
            for k in range(blocks):
                piece = jnp.broadcast_to(wave[:, k * LANES : (k + 1) * LANES], (LANES, LANES))
                turned.append(pltpu.roll(piece, 0, 1, stride=1, stride_axis=0))
            diag = [
                jnp.where(later, turned[k], turned[k - 1] if k else 0.0).astype(BF16)
                for k in range(blocks)
            ]
            matrix = jnp.concatenate(
                [
                    jnp.concatenate([nothing] * i + diag[: blocks - i], axis=1)
                    for i in range(blocks)
                ],
                axis=0,
            )
            field = jnp.concatenate([all_green[s, t] for t in range(tiles)], axis=1)
            total = total + jnp.dot(matrix, field, preferred_element_type=F32)
        adjoint[e] = total

    spot = lax.broadcasted_iota(jnp.int32, (nt, LANES), 1)

    def meet(j):
        part = jnp.zeros((1, LANES), F32)
        tile = 0
        for e in range(local_events):
            for a in range(full):
                field = all_strain[j, tile].astype(F32)
                one = adjoint[j * local_events + e, :, a * LANES : (a + 1) * LANES]
                part = part + jnp.sum(field * one, axis=0, keepdims=True)
                tile += 1
        if rest:
            for e in range(0, local_events, fit):
                field = all_strain[j, tile].astype(F32)
                one = adjoint[j * local_events + e, :, full * LANES :]
                for i in range(1, fit):
                    other = adjoint[j * local_events + e + i, :, full * LANES :]
                    one = jnp.where(spot < i * rest * width, one, other)
                part = part + jnp.sum(
                    jnp.where(spot < fit * rest * width, field * one, 0.0), axis=0, keepdims=True
                )
                tile += 1
        return part

    answer = meet(me)
    for d in order:
        j = peer(d)
        wait_from(2, all_strain, j)
        answer = answer + meet(j)
    total = answer[:, :width]
    for k in range(1, per_tile):
        total = total + answer[:, k * width : (k + 1) * width]
    out_ref[...] = total[0]
    for copy in copies:
        copy.wait_send()


def square_kernel(
    events_ref, counts_ref, resid_ref, green_hbm, strain_hbm, out_ref,
    green, strain, send_green, send_strain, own_green, far_green, own_strain, far_strain,
    own_tail, far_tail, waves, own_adjoint, far_adjoint, part_out, part_in,
    load_sem, send_sem, recv_sem,
):
    me = lax.axis_index("sta")
    x, y = lax.rem(me, 2), me // 2
    odd = lax.rem(x + y, 2)
    beside = me + 1 - 2 * x
    above = lax.rem(me + 2, 4)
    first = beside + odd * (above - beside)
    second = above + odd * (beside - above)
    across = 3 - me
    comps, nt, vox = green.shape
    local_events = strain.shape[0]
    width = vox // 4
    per_tile = LANES // width
    full = comps // per_tile
    rest = comps % per_tile
    blocks = nt // LANES
    head = full * nt

    load_green = pltpu.make_async_copy(green_hbm.at[0], green, load_sem.at[0])
    load_strain = pltpu.make_async_copy(strain_hbm, strain, load_sem.at[1])
    load_green.start()
    load_strain.start()

    barrier = pltpu.get_barrier_semaphore()
    for target in (first, second, across):
        pl.semaphore_signal(
            barrier, inc=1, device_id={"sta": target}, device_id_type=pl.DeviceIdType.MESH
        )

    def copy_of(kind, src, dst, target):
        return pltpu.make_async_remote_copy(
            src_ref=src,
            dst_ref=dst,
            send_sem=send_sem.at[kind],
            recv_sem=recv_sem.at[kind],
            device_id={"sta": target},
            device_id_type=pl.DeviceIdType.MESH,
        )

    plan = {
        "wave1": copy_of(0, waves.at[0], waves.at[2], first),
        "wave2": copy_of(1, waves.at[0], waves.at[1], second),
        "wave3": copy_of(2, waves.at[0], waves.at[3], across),
        "u0": copy_of(3, send_green.at[0], far_green.at[2], first),
        "u1": copy_of(4, send_strain.at[0], far_strain.at[1], first),
        "u2": copy_of(5, far_green.at[0], own_green.at[2], first),
        "u3": copy_of(6, far_green.at[2], own_green.at[3], first),
        "w0": copy_of(7, own_green.at[0], far_green.at[1], second),
        "w1": copy_of(8, send_green.at[1], own_green.at[1], second),
        "w2": copy_of(9, send_strain.at[1], own_strain.at[1], second),
        "w4": copy_of(10, own_green.at[1], far_green.at[3], second),
        "sum": copy_of(11, part_out, part_in, first),
    }

    events = waves.shape[1]
    rows = lax.broadcasted_iota(jnp.int32, (events, nt), 0)
    comb = jnp.zeros((events, nt), F32)
    for p in range(resid_ref.shape[0]):
        event = jnp.where(p < counts_ref[0], events_ref[0, p], -1)
        comb = comb + jnp.where(rows == event, resid_ref[p : p + 1, :], 0.0)
    waves[0] = comb

    lane = lax.broadcasted_iota(jnp.int32, (LANES, LANES), 0)
    column = lax.broadcasted_iota(jnp.int32, (LANES, LANES), 1)

    def picker(j):
        parts = []
        for slot in range(per_tile):
            inside = (column >= slot * width) & (column < (slot + 1) * width)
            hit = inside & (lane == column + (j - slot) * width)
            parts.append(jnp.where(hit, 1.0, 0.0).astype(BF16))
        return jnp.concatenate(parts, axis=0)

    def gathered(pieces, matrix):
        wide = jnp.concatenate(pieces, axis=1)
        return jnp.dot(wide, matrix, preferred_element_type=F32).astype(BF16)

    def pack_green(matrix, dst, index):
        for a in range(full):
            dst[index, a * nt : (a + 1) * nt] = gathered(
                [green[a * per_tile + k] for k in range(per_tile)], matrix
            )
        half = nt // 2
        dst[index, head : head + half] = gathered(
            [green[full * per_tile + k, h * half : (h + 1) * half] for h in range(2) for k in range(rest)],
            matrix,
        )

    def pack_strain(matrix, dst, index):
        tile = 0
        for e in range(local_events):
            for a in range(full):
                dst[index, tile] = gathered(
                    [strain[e, a * per_tile + k] for k in range(per_tile)], matrix
                )
                tile += 1
        dst[index, tile] = gathered(
            [strain[i, full * per_tile + k] for i in range(local_events) for k in range(rest)],
            matrix,
        )

    to_across, to_second = picker(across), picker(second)
    load_green.wait()
    pack_green(to_across, send_green, 0)
    pack_green(to_second, send_green, 1)
    to_me, to_first = picker(me), picker(first)
    pl.semaphore_wait(barrier, 3)
    plan["u0"].start()
    plan["w1"].start()
    for name in ("wave3", "wave1", "wave2"):
        plan[name].start()
    load_strain.wait()
    pack_strain(to_across, send_strain, 0)
    pack_green(to_me, own_green, 0)
    plan["u1"].start()
    pack_green(to_first, far_green, 0)
    plan["w0"].start()
    pack_strain(to_second, send_strain, 1)
    plan["u2"].start()

    later = column >= lane
    low = column < rest * width
    nothing = jnp.zeros((LANES, LANES), BF16)

    def unfold(source, s, dst):
        half = nt // 2
        for b in range(half // LANES):
            piece = source[s, head + b * LANES : head + (b + 1) * LANES].astype(F32)
            turned = pltpu.roll(piece, LANES // 2, 1)
            dst[s, b * LANES : (b + 1) * LANES] = jnp.where(low, piece, turned).astype(BF16)
            dst[s, half + b * LANES : half + (b + 1) * LANES] = jnp.where(
                low, turned, piece
            ).astype(BF16)

    def toeplitz(s, row):
        wave = waves[s, pl.ds(row, 1), :]
        turned = []
        for k in range(blocks):
            piece = jnp.broadcast_to(wave[:, k * LANES : (k + 1) * LANES], (LANES, LANES))
            turned.append(pltpu.roll(piece, 0, 1, stride=1, stride_axis=0))
        diag = [
            jnp.where(later, turned[k], turned[k - 1] if k else 0.0).astype(BF16)
            for k in range(blocks)
        ]
        return jnp.concatenate(
            [jnp.concatenate([nothing] * i + diag[: blocks - i], axis=1) for i in range(blocks)],
            axis=0,
        )

    def advance(source, tail, adjoint, partner, stations, fresh):
        for s in stations:
            unfold(source, s, tail)

        @pl.loop(0, 2 * local_events)
        def _(k):
            row = me * local_events + k + (k // local_events) * (partner - me - 1) * local_events
            total = jnp.zeros(adjoint.shape[1:], F32) if fresh else adjoint[k]
            for s in stations:
                field = jnp.concatenate(
                    [source[s, a * nt : (a + 1) * nt] for a in range(full)] + [tail[s]], axis=1
                )
                total = total + jnp.dot(toeplitz(s, row), field, preferred_element_type=F32)
            adjoint[k] = total

    spot = lax.broadcasted_iota(jnp.int32, (nt, LANES), 1)

    def meet(field, adjoint, side):
        part = jnp.zeros((1, LANES), F32)
        tile = 0
        base = side * local_events
        for e in range(local_events):
            for a in range(full):
                one = adjoint[base + e, :, a * LANES : (a + 1) * LANES]
                part = part + jnp.sum(field[side, tile].astype(F32) * one, axis=0, keepdims=True)
                tile += 1
        one = adjoint[base, :, full * LANES :]
        for i in range(1, local_events):
            one = jnp.where(spot < i * rest * width, one, adjoint[base + i, :, full * LANES :])
        return part + jnp.sum(field[side, tile].astype(F32) * one, axis=0, keepdims=True)

    plan["u0"].wait_recv()
    plan["u3"].start()
    plan["w1"].wait_recv()
    plan["w4"].start()
    plan["w2"].start()
    pack_strain(to_first, far_strain, 0)
    pack_strain(to_me, own_strain, 0)
    for name in ("wave1", "wave2", "wave3"):
        plan[name].wait_recv()
    advance(own_green, own_tail, own_adjoint, first, (0, 1), True)
    plan["w0"].wait_recv()
    advance(far_green, far_tail, far_adjoint, second, (0, 1, 2), True)
    plan["w4"].wait_recv()
    advance(far_green, far_tail, far_adjoint, second, (3,), False)
    part = meet(far_strain, far_adjoint, 0)
    plan["u1"].wait_recv()
    part_out[...] = part + meet(far_strain, far_adjoint, 1)
    plan["u2"].wait_recv()
    advance(own_green, own_tail, own_adjoint, first, (2,), False)
    plan["sum"].start()
    plan["u3"].wait_recv()
    advance(own_green, own_tail, own_adjoint, first, (3,), False)
    answer = meet(own_strain, own_adjoint, 0)
    plan["w2"].wait_recv()
    answer = answer + meet(own_strain, own_adjoint, 1)
    plan["sum"].wait_recv()
    answer = answer + part_in[...]
    total = answer[:, :width]
    for k in range(1, per_tile):
        total = total + answer[:, k * width : (k + 1) * width]
    out_ref[...] = total[0]
    for copy in plan.values():
        copy.wait_send()


def solution(mesh):
    n = mesh.shape["sta"]

    def body(green_tensor, strain, pair_events, pair_counts, residuals):
        _, comps, nt, vox = green_tensor.shape
        local_events = strain.shape[0]
        width = vox // n
        per_tile = LANES // width
        full = comps // per_tile
        rest = comps % per_tile
        fit = min(per_tile // rest, local_events) if rest else 1
        green_tiles = full + (1 if rest else 0)
        strain_tiles = full * local_events + (local_events // fit if rest else 0)
        events = n * local_events
        packed = full * nt + nt // 2
        if n == 4 and 2 * rest == per_tile and local_events * rest == per_tile:
            steps = square_kernel
            scratch = [
                pltpu.VMEM((comps, nt, vox), BF16),
                pltpu.VMEM((local_events, comps, nt, vox), BF16),
                pltpu.VMEM((2, packed, LANES), BF16),
                pltpu.VMEM((2, strain_tiles, nt, LANES), BF16),
                pltpu.VMEM((4, packed, LANES), BF16),
                pltpu.VMEM((4, packed, LANES), BF16),
                pltpu.VMEM((2, strain_tiles, nt, LANES), BF16),
                pltpu.VMEM((2, strain_tiles, nt, LANES), BF16),
                pltpu.VMEM((4, nt, LANES), BF16),
                pltpu.VMEM((4, nt, LANES), BF16),
                pltpu.VMEM((4, events, nt), F32),
                pltpu.VMEM((2 * local_events, nt, green_tiles * LANES), F32),
                pltpu.VMEM((2 * local_events, nt, green_tiles * LANES), F32),
                pltpu.VMEM((1, LANES), F32),
                pltpu.VMEM((1, LANES), F32),
                pltpu.SemaphoreType.DMA((2,)),
                pltpu.SemaphoreType.DMA((12,)),
                pltpu.SemaphoreType.DMA((12,)),
            ]
        else:
            steps = functools.partial(kernel, n)
            scratch = [
                pltpu.VMEM((comps, nt, vox), BF16),
                pltpu.VMEM((local_events, comps, nt, vox), BF16),
                pltpu.VMEM((n, green_tiles, nt, LANES), BF16),
                pltpu.VMEM((n, strain_tiles, nt, LANES), BF16),
                pltpu.VMEM((n, events, nt), F32),
                pltpu.VMEM((n, green_tiles, nt, LANES), BF16),
                pltpu.VMEM((n, strain_tiles, nt, LANES), BF16),
                pltpu.VMEM((events, nt, green_tiles * LANES), F32),
                pltpu.SemaphoreType.DMA((2,)),
                pltpu.SemaphoreType.DMA((3, n)),
                pltpu.SemaphoreType.DMA((3, n)),
            ]
        return pl.pallas_call(
            steps,
            out_shape=jax.ShapeDtypeStruct((width,), F32),
            in_specs=[
                pl.BlockSpec(memory_space=pltpu.SMEM),
                pl.BlockSpec(memory_space=pltpu.SMEM),
                pl.BlockSpec(memory_space=pltpu.VMEM),
                pl.BlockSpec(memory_space=pl.ANY),
                pl.BlockSpec(memory_space=pl.ANY),
            ],
            out_specs=pl.BlockSpec(memory_space=pltpu.VMEM),
            scratch_shapes=scratch,
            compiler_params=pltpu.CompilerParams(collective_id=0, has_side_effects=True),
        )(pair_events, pair_counts, residuals[0], green_tensor, strain)

    in_specs = (
        P("sta", None, None, "vox"),
        P("sta", None, None, "vox"),
        P("sta", None),
        P("sta"),
        P("sta", None, None),
    )
    out_specs = P(("vox", "sta"))
    return jax.shard_map(body, mesh=mesh, in_specs=in_specs, out_specs=out_specs, check_vma=False)
```

profile of v0, /device:TPU:0, one launch (start us, length us, event | category | flops | bytes accessed | tf_op | source)
XLA Modules:
  0.0 22.2 jit_solution(11258413603245625632)
XLA Ops:
  0.7 20.4 %shard_map.55 = f32[32]{0:T(128)} custom-call(s32[1,8]{1,0:T(1,128)} %events_ref.1, s32[1]{0:T(128)S(6)} %copy.7.counts_ref, f32[8,256]{1,0:T(8,128)} %bitcast.1, bf16[1,6,256,128]{3,2,1,0:T(8,128)(2,1)} %green_hbm.1, bf16[2,6,256,128]{3,2,1,0:T(8,128)(2,1)} %strain_hbm.1), custom_call_target="tpu_custom_call" | custom-call | tf_op jit(solution)/shard_map/pallas_call | solution.py:491
  21.0 1.2 %copy.8 = f32[32]{0:T(128)} copy(f32[32]{0:T(128)} %shard_map.55) | data formatting | bytes 256
where the time goes:
time: 22.5 us; the launch traced here: 22.2 us
  Pallas kernels  20.4 us (91%)
  local copies, waits for them, and re-layouts  1.19 us (5%)
  between operations  0.66 us (3%)
    pallas_call x1, Pallas kernels, body(): pl.pallas_call(steps, out_shape=jax.ShapeDtypeStruct((width,), F32), in_s...  20.4 us
    unnamed x1, local copies, waits for them, and re-layouts  1.19 us

commit v1 on v0

--- a/solution.py
+++ b/solution.py
@@ -217,10 +217,10 @@
 
 
 def square_kernel(
-    events_ref, counts_ref, resid_ref, green_hbm, strain_hbm, out_ref,
-    green, strain, send_green, send_strain, own_green, far_green, own_strain, far_strain,
-    own_tail, far_tail, waves, own_adjoint, far_adjoint, part_out, part_in,
-    load_sem, send_sem, recv_sem,
+    events_hbm, counts_hbm, resid_hbm, green_hbm, strain_hbm, out_ref,
+    events_ref, counts_ref, resid, own_head, far_head, own_field, far_field, raw_green, raw_strain,
+    send_tail, own_tail, far_tail, send_bits, own_bits, far_bits, waves, toeplitz, own_wide, far_wide,
+    early, head_sum, tail_sum, load_sem, send_sem, recv_sem,
 ):
     me = lax.axis_index("sta")
     x, y = lax.rem(me, 2), me // 2
@@ -230,61 +230,73 @@
     first = beside + odd * (above - beside)
     second = above + odd * (beside - above)
     across = 3 - me
-    comps, nt, vox = green.shape
-    local_events = strain.shape[0]
+    rest, nt, vox = raw_green.shape
+    local_events = raw_strain.shape[0]
+    events = waves.shape[1]
     width = vox // 4
     per_tile = LANES // width
-    full = comps // per_tile
-    rest = comps % per_tile
-    blocks = nt // LANES
-    head = full * nt
-
-    load_green = pltpu.make_async_copy(green_hbm.at[0], green, load_sem.at[0])
-    load_strain = pltpu.make_async_copy(strain_hbm, strain, load_sem.at[1])
-    load_green.start()
-    load_strain.start()
+    half = nt // 2
 
     barrier = pltpu.get_barrier_semaphore()
-    for target in (first, second, across):
+    for target in (first, second):
         pl.semaphore_signal(
             barrier, inc=1, device_id={"sta": target}, device_id_type=pl.DeviceIdType.MESH
         )
 
-    def copy_of(kind, src, dst, target):
-        return pltpu.make_async_remote_copy(
+    loads = {}
+    for name, src, dst in (
+        ("events", events_hbm, events_ref),
+        ("counts", counts_hbm, counts_ref),
+        ("resid", resid_hbm, resid),
+        ("green", green_hbm.at[0, pl.ds(4, rest)], raw_green),
+        ("strain", strain_hbm.at[:, pl.ds(4, rest)], raw_strain),
+        ("own_head", green_hbm.at[0, me], own_head.at[0]),
+        ("far_head", green_hbm.at[0, first], far_head.at[0]),
+        ("own_field", strain_hbm.at[:, me], own_field.at[0]),
+        ("far_field", strain_hbm.at[:, first], far_field.at[0]),
+    ):
+        loads[name] = pltpu.make_async_copy(src, dst, load_sem.at[len(loads)])
+        loads[name].start()
+
+    plan = {}
+    for name, src, dst, target in (
+        ("u0h", green_hbm.at[0, across], far_head.at[2], first),
+        ("u2h", green_hbm.at[0, first], own_head.at[2], first),
+        ("u1h", strain_hbm.at[:, across], far_field.at[1], first),
+        ("u3h", far_head.at[2], own_head.at[3], first),
+        ("w1h", green_hbm.at[0, second], own_head.at[1], second),
+        ("w0h", green_hbm.at[0, me], far_head.at[1], second),
+        ("w2h", strain_hbm.at[:, second], own_field.at[1], second),
+        ("w4h", own_head.at[1], far_head.at[3], second),
+        ("wave1", waves.at[0], waves.at[2], first),
+        ("wave2", waves.at[0], waves.at[1], second),
+        ("wave3", waves.at[2], waves.at[3], first),
+        ("u0t", send_tail.at[0], far_tail.at[2], first),
+        ("u2t", far_tail.at[0], own_tail.at[2], first),
+        ("u1t", send_bits.at[0], far_bits.at[1], first),
+        ("u3t", far_tail.at[2], own_tail.at[3], first),
+        ("w1t", send_tail.at[1], own_tail.at[1], second),
+        ("w0t", own_tail.at[0], far_tail.at[1], second),
+        ("w2t", send_bits.at[1], own_bits.at[1], second),
+        ("w4t", own_tail.at[1], far_tail.at[3], second),
+        ("head1", head_sum.at[0], head_sum.at[2], first),
+        ("head2", head_sum.at[0], head_sum.at[1], second),
+        ("head3", head_sum.at[0], head_sum.at[3], across),
+        ("tail", tail_sum.at[0], tail_sum.at[1], first),
+    ):
+        plan[name] = pltpu.make_async_remote_copy(
             src_ref=src,
             dst_ref=dst,
-            send_sem=send_sem.at[kind],
-            recv_sem=recv_sem.at[kind],
+            send_sem=send_sem.at[len(plan)],
+            recv_sem=recv_sem.at[len(plan)],
             device_id={"sta": target},
             device_id_type=pl.DeviceIdType.MESH,
         )
 
-    plan = {
-        "wave1": copy_of(0, waves.at[0], waves.at[2], first),
-        "wave2": copy_of(1, waves.at[0], waves.at[1], second),
-        "wave3": copy_of(2, waves.at[0], waves.at[3], across),
-        "u0": copy_of(3, send_green.at[0], far_green.at[2], first),
-        "u1": copy_of(4, send_strain.at[0], far_strain.at[1], first),
-        "u2": copy_of(5, far_green.at[0], own_green.at[2], first),
-        "u3": copy_of(6, far_green.at[2], own_green.at[3], first),
-        "w0": copy_of(7, own_green.at[0], far_green.at[1], second),
-        "w1": copy_of(8, send_green.at[1], own_green.at[1], second),
-        "w2": copy_of(9, send_strain.at[1], own_strain.at[1], second),
-        "w4": copy_of(10, own_green.at[1], far_green.at[3], second),
-        "sum": copy_of(11, part_out, part_in, first),
-    }
-
-    events = waves.shape[1]
-    rows = lax.broadcasted_iota(jnp.int32, (events, nt), 0)
-    comb = jnp.zeros((events, nt), F32)
-    for p in range(resid_ref.shape[0]):
-        event = jnp.where(p < counts_ref[0], events_ref[0, p], -1)
-        comb = comb + jnp.where(rows == event, resid_ref[p : p + 1, :], 0.0)
-    waves[0] = comb
-
     lane = lax.broadcasted_iota(jnp.int32, (LANES, LANES), 0)
     column = lax.broadcasted_iota(jnp.int32, (LANES, LANES), 1)
+    later = column >= lane
+    low = column < LANES // 2
 
     def picker(j):
         parts = []
@@ -294,140 +306,153 @@
             parts.append(jnp.where(hit, 1.0, 0.0).astype(BF16))
         return jnp.concatenate(parts, axis=0)
 
-    def gathered(pieces, matrix):
-        wide = jnp.concatenate(pieces, axis=1)
+    def folded(source, matrix):
+        wide = jnp.concatenate(
+            [source[k, h * half : (h + 1) * half] for h in range(2) for k in range(rest)], axis=1
+        )
         return jnp.dot(wide, matrix, preferred_element_type=F32).astype(BF16)
 
-    def pack_green(matrix, dst, index):
-        for a in range(full):
-            dst[index, a * nt : (a + 1) * nt] = gathered(
-                [green[a * per_tile + k] for k in range(per_tile)], matrix
+    def make_toeplitz(s):
+        @pl.loop(0, 3 * local_events)
+        def _(k):
+            group = k // local_events
+            owner = me + (group % 2) * (first - me) + (group // 2) * (second - me)
+            wave = waves[s, pl.ds(owner * local_events + k - group * local_events, 1), :]
+            before = 0.0
+            for b in range(2):
+                piece = jnp.broadcast_to(wave[:, b * LANES : (b + 1) * LANES], (LANES, LANES))
+                turned = pltpu.roll(piece, 0, 1, stride=1, stride_axis=0)
+                toeplitz[k, s, b] = jnp.where(later, turned, before).astype(BF16)
+                before = turned
+
+    def widen(source, s, dst):
+        piece = source[s].astype(F32)
+        dst[s, :half] = source[s]
+        dst[s, half:] = jnp.where(low, pltpu.roll(piece, LANES // 2, 1), 0.0).astype(BF16)
+
+    to_across, to_second, to_me, to_first = (picker(j) for j in (across, second, me, first))
+
+    pl.semaphore_wait(barrier, 2)
+    for name in ("u0h", "w1h", "u2h", "w0h"):
+        plan[name].start()
+
+    for name in ("events", "counts", "resid"):
+        loads[name].wait()
+    rows = lax.broadcasted_iota(jnp.int32, (events, nt), 0)
+    comb = jnp.zeros((events, nt), F32)
+    for p in range(resid.shape[1]):
+        event = jnp.where(p < counts_ref[0], events_ref[0, p], -1)
+        comb = comb + jnp.where(rows == event, resid[0, p : p + 1, :], 0.0)
+    waves[0] = comb
+
+    loads["green"].wait()
+    send_tail[0] = folded(raw_green, to_across)
+    send_tail[1] = folded(raw_green, to_second)
+    for name in ("wave1", "wave2", "u0t", "w1t", "u1h", "w2h"):
+        plan[name].start()
+    far_tail[0] = folded(raw_green, to_first)
+    own_tail[0] = folded(raw_green, to_me)
+    loads["strain"].wait()
+    for e in range(local_events):
+        send_bits[0, e] = folded(raw_strain.at[e], to_across)
+        send_bits[1, e] = folded(raw_strain.at[e], to_second)
+    make_toeplitz(0)
+    plan["u0h"].wait_recv()
+    plan["u3h"].start()
+    plan["w1h"].wait_recv()
+    plan["w4h"].start()
+    plan["wave1"].wait_recv()
+    plan["wave3"].start()
+    for name in ("u1t", "w0t", "u2t"):
+        plan[name].start()
+    for e in range(local_events):
+        far_bits[0, e] = folded(raw_strain.at[e], to_first)
+        own_bits[0, e] = folded(raw_strain.at[e], to_me)
+    make_toeplitz(2)
+    plan["wave2"].wait_recv()
+    make_toeplitz(1)
+    plan["u0t"].wait_recv()
+    plan["u3t"].start()
+    plan["w1t"].wait_recv()
+    plan["w4t"].start()
+    plan["w2t"].start()
+    plan["wave3"].wait_recv()
+    make_toeplitz(3)
+    for s in range(3):
+        if s < 2:
+            widen(own_tail, s, own_wide)
+        if s != 1:
+            widen(far_tail, s, far_wide)
+
+    def head_matrix(k):
+        nothing = jnp.zeros((half, half), BF16)
+        top = [toeplitz[k, s, b] for s in range(4) for b in range(2)]
+        bottom = [piece for s in range(4) for piece in (nothing, toeplitz[k, s, 0])]
+        return jnp.concatenate(
+            [jnp.concatenate(top, axis=1), jnp.concatenate(bottom, axis=1)], axis=0
+        )
+
+    def tail_matrix(k, stations):
+        return jnp.concatenate([toeplitz[k, s, b] for s in stations for b in range(2)], axis=1)
+
+    def met(field, adjoint):
+        return jnp.sum(field.astype(F32) * adjoint, axis=0, keepdims=True)
+
+    for name in ("own_head", "far_head", "own_field", "far_field"):
+        loads[name].wait()
+    for name in ("u2h", "w0h", "u1h", "w2h", "u3h", "w4h"):
+        plan[name].wait_recv()
+    own_stack = jnp.concatenate([own_head[s] for s in range(4)], axis=0)
+    far_stack = jnp.concatenate([far_head[s] for s in range(4)], axis=0)
+    both_stack = jnp.concatenate([own_stack, far_stack], axis=1)
+    part = jnp.zeros((1, LANES), F32)
+    for e in range(local_events):
+        both = jnp.dot(head_matrix(e), both_stack, preferred_element_type=F32)
+        part = part + met(own_field[0, e], both[:, :LANES]) + met(far_field[0, e], both[:, LANES:])
+        one = jnp.dot(head_matrix(local_events + e), own_stack, preferred_element_type=F32)
+        part = part + met(own_field[1, e], one)
+        one = jnp.dot(head_matrix(2 * local_events + e), far_stack, preferred_element_type=F32)
+        part = part + met(far_field[1, e], one)
+    head_sum[0] = part
+    for name in ("head3", "head1", "head2"):
+        plan[name].start()
+
+    for name in ("w0t", "u1t", "w4t"):
+        plan[name].wait_recv()
+    widen(far_tail, 1, far_wide)
+    widen(far_tail, 3, far_wide)
+    far_rhs = jnp.concatenate([far_wide[s] for s in range(4)], axis=0)
+    part = jnp.zeros((1, LANES), F32)
+    for g, side in ((0, 0), (2, 1)):
+        for e in range(local_events):
+            k = g * local_events + e
+            one = jnp.dot(tail_matrix(k, range(4)), far_rhs, preferred_element_type=F32)
+            part = part + met(far_bits[side, e], one)
+    tail_sum[0] = part
+    plan["tail"].start()
+
+    plan["u2t"].wait_recv()
+    widen(own_tail, 2, own_wide)
+    own_rhs = jnp.concatenate([own_wide[s] for s in range(3)], axis=0)
+    for k in range(2 * local_events):
+        early[k] = jnp.dot(tail_matrix(k, range(3)), own_rhs, preferred_element_type=F32)
+    plan["u3t"].wait_recv()
+    widen(own_tail, 3, own_wide)
+    plan["w2t"].wait_recv()
+    part = jnp.zeros((1, LANES), F32)
+    for g in range(2):
+        for e in range(local_events):
+            k = g * local_events + e
+            one = early[k] + jnp.dot(
+                tail_matrix(k, (3,)), own_wide[3], preferred_element_type=F32
             )
-        half = nt // 2
-        dst[index, head : head + half] = gathered(
-            [green[full * per_tile + k, h * half : (h + 1) * half] for h in range(2) for k in range(rest)],
-            matrix,
-        )
-
-    def pack_strain(matrix, dst, index):
-        tile = 0
-        for e in range(local_events):
-            for a in range(full):
-                dst[index, tile] = gathered(
-                    [strain[e, a * per_tile + k] for k in range(per_tile)], matrix
-                )
-                tile += 1
-        dst[index, tile] = gathered(
-            [strain[i, full * per_tile + k] for i in range(local_events) for k in range(rest)],
-            matrix,
-        )
-
-    to_across, to_second = picker(across), picker(second)
-    load_green.wait()
-    pack_green(to_across, send_green, 0)
-    pack_green(to_second, send_green, 1)
-    to_me, to_first = picker(me), picker(first)
-    pl.semaphore_wait(barrier, 3)
-    plan["u0"].start()
-    plan["w1"].start()
-    for name in ("wave3", "wave1", "wave2"):
-        plan[name].start()
-    load_strain.wait()
-    pack_strain(to_across, send_strain, 0)
-    pack_green(to_me, own_green, 0)
-    plan["u1"].start()
-    pack_green(to_first, far_green, 0)
-    plan["w0"].start()
-    pack_strain(to_second, send_strain, 1)
-    plan["u2"].start()
-
-    later = column >= lane
-    low = column < rest * width
-    nothing = jnp.zeros((LANES, LANES), BF16)
-
-    def unfold(source, s, dst):
-        half = nt // 2
-        for b in range(half // LANES):
-            piece = source[s, head + b * LANES : head + (b + 1) * LANES].astype(F32)
-            turned = pltpu.roll(piece, LANES // 2, 1)
-            dst[s, b * LANES : (b + 1) * LANES] = jnp.where(low, piece, turned).astype(BF16)
-            dst[s, half + b * LANES : half + (b + 1) * LANES] = jnp.where(
-                low, turned, piece
-            ).astype(BF16)
-
-    def toeplitz(s, row):
-        wave = waves[s, pl.ds(row, 1), :]
-        turned = []
-        for k in range(blocks):
-            piece = jnp.broadcast_to(wave[:, k * LANES : (k + 1) * LANES], (LANES, LANES))
-            turned.append(pltpu.roll(piece, 0, 1, stride=1, stride_axis=0))
-        diag = [
-            jnp.where(later, turned[k], turned[k - 1] if k else 0.0).astype(BF16)
-            for k in range(blocks)
-        ]
-        return jnp.concatenate(
-            [jnp.concatenate([nothing] * i + diag[: blocks - i], axis=1) for i in range(blocks)],
-            axis=0,
-        )
-
-    def advance(source, tail, adjoint, partner, stations, fresh):
-        for s in stations:
-            unfold(source, s, tail)
-
-        @pl.loop(0, 2 * local_events)
-        def _(k):
-            row = me * local_events + k + (k // local_events) * (partner - me - 1) * local_events
-            total = jnp.zeros(adjoint.shape[1:], F32) if fresh else adjoint[k]
-            for s in stations:
-                field = jnp.concatenate(
-                    [source[s, a * nt : (a + 1) * nt] for a in range(full)] + [tail[s]], axis=1
-                )
-                total = total + jnp.dot(toeplitz(s, row), field, preferred_element_type=F32)
-            adjoint[k] = total
-
-    spot = lax.broadcasted_iota(jnp.int32, (nt, LANES), 1)
-
-    def meet(field, adjoint, side):
-        part = jnp.zeros((1, LANES), F32)
-        tile = 0
-        base = side * local_events
-        for e in range(local_events):
-            for a in range(full):
-                one = adjoint[base + e, :, a * LANES : (a + 1) * LANES]
-                part = part + jnp.sum(field[side, tile].astype(F32) * one, axis=0, keepdims=True)
-                tile += 1
-        one = adjoint[base, :, full * LANES :]
-        for i in range(1, local_events):
-            one = jnp.where(spot < i * rest * width, one, adjoint[base + i, :, full * LANES :])
-        return part + jnp.sum(field[side, tile].astype(F32) * one, axis=0, keepdims=True)
-
-    plan["u0"].wait_recv()
-    plan["u3"].start()
-    plan["w1"].wait_recv()
-    plan["w4"].start()
-    plan["w2"].start()
-    pack_strain(to_first, far_strain, 0)
-    pack_strain(to_me, own_strain, 0)
-    for name in ("wave1", "wave2", "wave3"):
+            part = part + met(own_bits[g, e], one)
+    for name in ("head1", "head2", "head3", "tail"):
         plan[name].wait_recv()
-    advance(own_green, own_tail, own_adjoint, first, (0, 1), True)
-    plan["w0"].wait_recv()
-    advance(far_green, far_tail, far_adjoint, second, (0, 1, 2), True)
-    plan["w4"].wait_recv()
-    advance(far_green, far_tail, far_adjoint, second, (3,), False)
-    part = meet(far_strain, far_adjoint, 0)
-    plan["u1"].wait_recv()
-    part_out[...] = part + meet(far_strain, far_adjoint, 1)
-    plan["u2"].wait_recv()
-    advance(own_green, own_tail, own_adjoint, first, (2,), False)
-    plan["sum"].start()
-    plan["u3"].wait_recv()
-    advance(own_green, own_tail, own_adjoint, first, (3,), False)
-    answer = meet(own_strain, own_adjoint, 0)
-    plan["w2"].wait_recv()
-    answer = answer + meet(own_strain, own_adjoint, 1)
-    plan["sum"].wait_recv()
-    answer = answer + part_in[...]
+    heads = head_sum[0] + head_sum[1] + head_sum[2] + head_sum[3]
+    spot = lax.broadcasted_iota(jnp.int32, (1, LANES), 1)
+    mine = (spot >= me * width) & (spot < (me + 1) * width)
+    answer = part + tail_sum[1] + jnp.where(mine, heads, 0.0)
     total = answer[:, :width]
     for k in range(1, per_tile):
         total = total + answer[:, k * width : (k + 1) * width]
@@ -450,28 +475,42 @@
         green_tiles = full + (1 if rest else 0)
         strain_tiles = full * local_events + (local_events // fit if rest else 0)
         events = n * local_events
-        packed = full * nt + nt // 2
-        if n == 4 and 2 * rest == per_tile and local_events * rest == per_tile:
+        pairs = pair_events.shape[1]
+        left = comps - n
+        square = n == 4 and nt == 2 * LANES and 0 < left and 2 * left == per_tile
+        if square:
             steps = square_kernel
+            half = nt // 2
+            head = (4, nt, LANES)
+            field = (2, local_events, nt, LANES)
+            tail = (4, half, LANES)
+            bits = (2, local_events, half, LANES)
             scratch = [
-                pltpu.VMEM((comps, nt, vox), BF16),
-                pltpu.VMEM((local_events, comps, nt, vox), BF16),
-                pltpu.VMEM((2, packed, LANES), BF16),
-                pltpu.VMEM((2, strain_tiles, nt, LANES), BF16),
-                pltpu.VMEM((4, packed, LANES), BF16),
-                pltpu.VMEM((4, packed, LANES), BF16),
-                pltpu.VMEM((2, strain_tiles, nt, LANES), BF16),
-                pltpu.VMEM((2, strain_tiles, nt, LANES), BF16),
-                pltpu.VMEM((4, nt, LANES), BF16),
-                pltpu.VMEM((4, nt, LANES), BF16),
+                pltpu.SMEM((1, pairs), jnp.int32),
+                pltpu.SMEM((1,), jnp.int32),
+                pltpu.VMEM((1, pairs, nt), F32),
+                pltpu.VMEM(head, BF16),
+                pltpu.VMEM(head, BF16),
+                pltpu.VMEM(field, BF16),
+                pltpu.VMEM(field, BF16),
+                pltpu.VMEM((left, nt, vox), BF16),
+                pltpu.VMEM((local_events, left, nt, vox), BF16),
+                pltpu.VMEM((2, half, LANES), BF16),
+                pltpu.VMEM(tail, BF16),
+                pltpu.VMEM(tail, BF16),
+                pltpu.VMEM(bits, BF16),
+                pltpu.VMEM(bits, BF16),
+                pltpu.VMEM(bits, BF16),
                 pltpu.VMEM((4, events, nt), F32),
-                pltpu.VMEM((2 * local_events, nt, green_tiles * LANES), F32),
-                pltpu.VMEM((2 * local_events, nt, green_tiles * LANES), F32),
-                pltpu.VMEM((1, LANES), F32),
-                pltpu.VMEM((1, LANES), F32),
-                pltpu.SemaphoreType.DMA((2,)),
-                pltpu.SemaphoreType.DMA((12,)),
-                pltpu.SemaphoreType.DMA((12,)),
+                pltpu.VMEM((3 * local_events, 4, 2, half, half), BF16),
+                pltpu.VMEM(head, BF16),
+                pltpu.VMEM(head, BF16),
+                pltpu.VMEM((2 * local_events, half, LANES), F32),
+                pltpu.VMEM((4, 1, LANES), F32),
+                pltpu.VMEM((2, 1, LANES), F32),
+                pltpu.SemaphoreType.DMA((9,)),
+                pltpu.SemaphoreType.DMA((23,)),
+                pltpu.SemaphoreType.DMA((23,)),
             ]
         else:
             steps = functools.partial(kernel, n)
@@ -488,6 +527,15 @@
                 pltpu.SemaphoreType.DMA((3, n)),
                 pltpu.SemaphoreType.DMA((3, n)),
             ]
+        if square:
+            return pl.pallas_call(
+                steps,
+                out_shape=pltpu.VMEM((width,), F32),
+                in_specs=[pl.BlockSpec(memory_space=pl.ANY)] * 5,
+                out_specs=pl.BlockSpec(memory_space=pltpu.VMEM),
+                scratch_shapes=scratch,
+                compiler_params=pltpu.CompilerParams(collective_id=0, has_side_effects=True),
+            )(pair_events, pair_counts, residuals, green_tensor, strain)
         return pl.pallas_call(
             steps,
             out_shape=jax.ShapeDtypeStruct((width,), F32),

time: 22.5 us -> 21 us (0.933)
  Pallas kernels: 20.4 us -> 19.7 us
  local copies, waits for them, and re-layouts: 1.19 us -> 0.51 us
    pallas_call x1, Pallas kernels: 20.4 us -> 19.7 us  [body(): pl.pallas_call(steps, out_shape=pltpu.VMEM((width,), F32), in_specs=[pl.B...]
    unnamed x1, local copies, waits for them, and re-layouts: 1.19 us -> 0.51 us
where the time goes in v1:
time: 21 us; the launch traced here: 20.8 us
  Pallas kernels  19.7 us (94%)
  between operations  0.66 us (3%)
  local copies, waits for them, and re-layouts  0.51 us (2%)
    pallas_call x1, Pallas kernels, body(): pl.pallas_call(steps, out_shape=pltpu.VMEM((width,), F32), in_specs=[pl.B...  19.7 us
    unnamed x1, local copies, waits for them, and re-layouts  0.51 us

profile of v1, /device:TPU:0, one launch (start us, length us, event | category | flops | bytes accessed | tf_op | source)
XLA Modules:
  0.0 20.8 jit_solution(7836102831943733943)
XLA Ops:
  0.7 19.7 %shard_map.55 = f32[32]{0:T(128)S(1)} custom-call(s32[1,8]{1,0:T(1,128)} %events_hbm.1, s32[1]{0:T(128)S(6)} %copy.8.counts_hbm, f32[1,8,256]{2,1,0:T(8,128)} %resid_hbm.1, bf16[1,6,256,128]{3,2,1,0:T(8,128)(2,1)} %green_hbm.1, bf16[2,6,256,128]{3,2,1,0:T(8,128)(2,1)} %strain_hbm.1), custom_call_target="tpu_custom_call" | custom-call | tf_op jit(solution)/shard_map/pallas_call | solution.py:531
  20.3 0.5 %copy.7 = f32[32]{0:T(128)} copy(f32[32]{0:T(128)S(1)} %shard_map.55) | data formatting | bytes 256

commit v2 on v1

--- a/solution.py
+++ b/solution.py
@@ -218,9 +218,10 @@
 
 def square_kernel(
     events_hbm, counts_hbm, resid_hbm, green_hbm, strain_hbm, out_ref,
-    events_ref, counts_ref, resid, own_head, far_head, own_field, far_field, raw_green, raw_strain,
-    send_tail, own_tail, far_tail, send_bits, own_bits, far_bits, waves, toeplitz, own_wide, far_wide,
-    early, head_sum, tail_sum, load_sem, send_sem, recv_sem,
+    events_ref, counts_ref, resid, green, strain,
+    send_head, own_head, far_head, send_field, own_field, far_field,
+    send_tail, own_tail, far_tail, send_bits, own_bits, far_bits, own_wide, far_wide,
+    waves, rows_of, toeplitz, head_sum, tail_sum, side_sum, load_sem, send_sem, recv_sem,
 ):
     me = lax.axis_index("sta")
     x, y = lax.rem(me, 2), me // 2
@@ -230,11 +231,12 @@
     first = beside + odd * (above - beside)
     second = above + odd * (beside - above)
     across = 3 - me
-    rest, nt, vox = raw_green.shape
-    local_events = raw_strain.shape[0]
+    comps, nt, vox = green.shape
+    local_events = strain.shape[0]
     events = waves.shape[1]
     width = vox // 4
     per_tile = LANES // width
+    rest = comps - per_tile
     half = nt // 2
 
     barrier = pltpu.get_barrier_semaphore()
@@ -245,44 +247,45 @@
 
     loads = {}
     for name, src, dst in (
+        ("green", green_hbm.at[0], green),
         ("events", events_hbm, events_ref),
         ("counts", counts_hbm, counts_ref),
         ("resid", resid_hbm, resid),
-        ("green", green_hbm.at[0, pl.ds(4, rest)], raw_green),
-        ("strain", strain_hbm.at[:, pl.ds(4, rest)], raw_strain),
-        ("own_head", green_hbm.at[0, me], own_head.at[0]),
-        ("far_head", green_hbm.at[0, first], far_head.at[0]),
-        ("own_field", strain_hbm.at[:, me], own_field.at[0]),
-        ("far_field", strain_hbm.at[:, first], far_field.at[0]),
+        ("strain", strain_hbm, strain),
     ):
         loads[name] = pltpu.make_async_copy(src, dst, load_sem.at[len(loads)])
         loads[name].start()
 
+    low_half, high_half = pl.ds(0, LANES), pl.ds(LANES, LANES)
     plan = {}
     for name, src, dst, target in (
-        ("u0h", green_hbm.at[0, across], far_head.at[2], first),
-        ("u2h", green_hbm.at[0, first], own_head.at[2], first),
-        ("u1h", strain_hbm.at[:, across], far_field.at[1], first),
+        ("u0h", send_head.at[0], far_head.at[2], first),
+        ("u2h", far_head.at[0], own_head.at[2], first),
         ("u3h", far_head.at[2], own_head.at[3], first),
-        ("w1h", green_hbm.at[0, second], own_head.at[1], second),
-        ("w0h", green_hbm.at[0, me], far_head.at[1], second),
-        ("w2h", strain_hbm.at[:, second], own_field.at[1], second),
+        ("w1h", send_head.at[1], own_head.at[1], second),
+        ("w0h", own_head.at[0], far_head.at[1], second),
         ("w4h", own_head.at[1], far_head.at[3], second),
-        ("wave1", waves.at[0], waves.at[2], first),
-        ("wave2", waves.at[0], waves.at[1], second),
-        ("wave3", waves.at[2], waves.at[3], first),
         ("u0t", send_tail.at[0], far_tail.at[2], first),
         ("u2t", far_tail.at[0], own_tail.at[2], first),
-        ("u1t", send_bits.at[0], far_bits.at[1], first),
         ("u3t", far_tail.at[2], own_tail.at[3], first),
         ("w1t", send_tail.at[1], own_tail.at[1], second),
         ("w0t", own_tail.at[0], far_tail.at[1], second),
-        ("w2t", send_bits.at[1], own_bits.at[1], second),
         ("w4t", own_tail.at[1], far_tail.at[3], second),
-        ("head1", head_sum.at[0], head_sum.at[2], first),
-        ("head2", head_sum.at[0], head_sum.at[1], second),
-        ("head3", head_sum.at[0], head_sum.at[3], across),
-        ("tail", tail_sum.at[0], tail_sum.at[1], first),
+        ("wave1", waves.at[0], waves.at[2], first),
+        ("wave2", waves.at[0], waves.at[1], second),
+        ("wave3", waves.at[2, :, low_half], waves.at[3, :, low_half], first),
+        ("wave4", waves.at[1, :, high_half], waves.at[3, :, high_half], second),
+        ("side", side_sum.at[0], side_sum.at[1], first),
+        *(
+            item
+            for e in range(local_events)
+            for item in (
+                (f"u1h{e}", send_field.at[0, e], far_field.at[1, e], first),
+                (f"w2h{e}", send_field.at[1, e], own_field.at[1, e], second),
+                (f"u1t{e}", send_bits.at[0, e], far_bits.at[1, e], first),
+                (f"w2t{e}", send_bits.at[1, e], own_bits.at[1, e], second),
+            )
+        ),
     ):
         plan[name] = pltpu.make_async_remote_copy(
             src_ref=src,
@@ -293,6 +296,15 @@
             device_id_type=pl.DeviceIdType.MESH,
         )
 
+    def start(*names):
+        for name in names:
+            plan[name].start()
+
+    def arrive(*names):
+        for name in names:
+            plan[name].wait_recv()
+
+    each = range(local_events)
     lane = lax.broadcasted_iota(jnp.int32, (LANES, LANES), 0)
     column = lax.broadcasted_iota(jnp.int32, (LANES, LANES), 1)
     later = column >= lane
@@ -306,18 +318,27 @@
             parts.append(jnp.where(hit, 1.0, 0.0).astype(BF16))
         return jnp.concatenate(parts, axis=0)
 
-    def folded(source, matrix):
-        wide = jnp.concatenate(
-            [source[k, h * half : (h + 1) * half] for h in range(2) for k in range(rest)], axis=1
+    def packed(pieces, matrix):
+        wide = jnp.concatenate(pieces, axis=1)
+        return jnp.dot(wide, matrix, preferred_element_type=F32).astype(BF16)
+
+    def head_of(source, matrix):
+        return packed([source[k] for k in range(per_tile)], matrix)
+
+    def tail_of(source, matrix):
+        return packed(
+            [source[per_tile + k, h * half : (h + 1) * half] for h in range(2) for k in range(rest)],
+            matrix,
         )
-        return jnp.dot(wide, matrix, preferred_element_type=F32).astype(BF16)
 
     def make_toeplitz(s):
+        rows_of[...] = waves[s].astype(F32)
+
         @pl.loop(0, 3 * local_events)
         def _(k):
             group = k // local_events
             owner = me + (group % 2) * (first - me) + (group // 2) * (second - me)
-            wave = waves[s, pl.ds(owner * local_events + k - group * local_events, 1), :]
+            wave = rows_of[pl.ds(owner * local_events + k - group * local_events, 1), :]
             before = 0.0
             for b in range(2):
                 piece = jnp.broadcast_to(wave[:, b * LANES : (b + 1) * LANES], (LANES, LANES))
@@ -330,11 +351,32 @@
         dst[s, :half] = source[s]
         dst[s, half:] = jnp.where(low, pltpu.roll(piece, LANES // 2, 1), 0.0).astype(BF16)
 
-    to_across, to_second, to_me, to_first = (picker(j) for j in (across, second, me, first))
-
+    nothing = jnp.zeros((half, half), BF16)
+
+    def head_dot(k, stations, heads):
+        top = [toeplitz[k, s, b] for s in stations for b in range(2)]
+        bottom = [piece for s in stations for piece in (nothing, toeplitz[k, s, 0])]
+        matrix = jnp.concatenate(
+            [jnp.concatenate(top, axis=1), jnp.concatenate(bottom, axis=1)], axis=0
+        )
+        stack = jnp.concatenate([heads[s] for s in stations], axis=0)
+        return jnp.dot(matrix, stack, preferred_element_type=F32)
+
+    def tail_dot(k, stations, wides):
+        matrix = jnp.concatenate([toeplitz[k, s, b] for s in stations for b in range(2)], axis=1)
+        stack = jnp.concatenate([wides[s] for s in stations], axis=0)
+        return jnp.dot(matrix, stack, preferred_element_type=F32)
+
+    def met(field, adjoint):
+        return jnp.sum(field.astype(F32) * adjoint, axis=0, keepdims=True)
+
+    to_across, to_second = picker(across), picker(second)
+    loads["green"].wait()
+    send_head[0] = head_of(green, to_across)
     pl.semaphore_wait(barrier, 2)
-    for name in ("u0h", "w1h", "u2h", "w0h"):
-        plan[name].start()
+    start("u0h")
+    send_head[1] = head_of(green, to_second)
+    start("w1h")
 
     for name in ("events", "counts", "resid"):
         loads[name].wait()
@@ -343,116 +385,104 @@
     for p in range(resid.shape[1]):
         event = jnp.where(p < counts_ref[0], events_ref[0, p], -1)
         comb = comb + jnp.where(rows == event, resid[0, p : p + 1, :], 0.0)
-    waves[0] = comb
-
-    loads["green"].wait()
-    send_tail[0] = folded(raw_green, to_across)
-    send_tail[1] = folded(raw_green, to_second)
-    for name in ("wave1", "wave2", "u0t", "w1t", "u1h", "w2h"):
-        plan[name].start()
-    far_tail[0] = folded(raw_green, to_first)
-    own_tail[0] = folded(raw_green, to_me)
+    waves[0] = comb.astype(BF16)
+    start("wave1", "wave2")
+
+    send_tail[0] = tail_of(green, to_across)
+    send_tail[1] = tail_of(green, to_second)
+    start("u0t", "w1t")
+    to_me, to_first = picker(me), picker(first)
+    own_head[0] = head_of(green, to_me)
     loads["strain"].wait()
-    for e in range(local_events):
-        send_bits[0, e] = folded(raw_strain.at[e], to_across)
-        send_bits[1, e] = folded(raw_strain.at[e], to_second)
+    send_field[0, 0] = head_of(strain.at[0], to_across)
+    start("w0h", "u1h0")
+    arrive("wave1", "wave2")
+    start("wave3", "wave4")
+    for e in each[1:]:
+        send_field[0, e] = head_of(strain.at[e], to_across)
+        start(f"u1h{e}")
+    own_tail[0] = tail_of(green, to_me)
+    for e in each:
+        send_bits[0, e] = tail_of(strain.at[e], to_across)
+    arrive("w1h")
+    start("w4h", "w0t")
+    for e in each:
+        start(f"u1t{e}")
+    arrive("w1t")
+    start("w4t")
+    far_head[0] = head_of(green, to_first)
+    start("u2h")
+    for e in each:
+        send_field[1, e] = head_of(strain.at[e], to_second)
+        start(f"w2h{e}")
+    arrive("u0h")
+    start("u3h")
+    far_tail[0] = tail_of(green, to_first)
+    for e in each:
+        send_bits[1, e] = tail_of(strain.at[e], to_second)
+        start(f"w2t{e}")
     make_toeplitz(0)
-    plan["u0h"].wait_recv()
-    plan["u3h"].start()
-    plan["w1h"].wait_recv()
-    plan["w4h"].start()
-    plan["wave1"].wait_recv()
-    plan["wave3"].start()
-    for name in ("u1t", "w0t", "u2t"):
-        plan[name].start()
-    for e in range(local_events):
-        far_bits[0, e] = folded(raw_strain.at[e], to_first)
-        own_bits[0, e] = folded(raw_strain.at[e], to_me)
+    make_toeplitz(1)
     make_toeplitz(2)
-    plan["wave2"].wait_recv()
-    make_toeplitz(1)
-    plan["u0t"].wait_recv()
-    plan["u3t"].start()
-    plan["w1t"].wait_recv()
-    plan["w4t"].start()
-    plan["w2t"].start()
-    plan["wave3"].wait_recv()
+    for e in each:
+        far_field[0, e] = head_of(strain.at[e], to_first)
+        far_bits[0, e] = tail_of(strain.at[e], to_first)
+        own_field[0, e] = head_of(strain.at[e], to_me)
+        own_bits[0, e] = tail_of(strain.at[e], to_me)
+    widen(own_tail, 0, own_wide)
+    widen(own_tail, 1, own_wide)
+    widen(far_tail, 0, far_wide)
+    arrive("u0t")
+    widen(far_tail, 2, far_wide)
+    arrive("wave3", "wave4")
+    start("u2t", "u3t")
     make_toeplitz(3)
-    for s in range(3):
-        if s < 2:
-            widen(own_tail, s, own_wide)
-        if s != 1:
-            widen(far_tail, s, far_wide)
-
-    def head_matrix(k):
-        nothing = jnp.zeros((half, half), BF16)
-        top = [toeplitz[k, s, b] for s in range(4) for b in range(2)]
-        bottom = [piece for s in range(4) for piece in (nothing, toeplitz[k, s, 0])]
-        return jnp.concatenate(
-            [jnp.concatenate(top, axis=1), jnp.concatenate(bottom, axis=1)], axis=0
-        )
-
-    def tail_matrix(k, stations):
-        return jnp.concatenate([toeplitz[k, s, b] for s in stations for b in range(2)], axis=1)
-
-    def met(field, adjoint):
-        return jnp.sum(field.astype(F32) * adjoint, axis=0, keepdims=True)
-
-    for name in ("own_head", "far_head", "own_field", "far_field"):
-        loads[name].wait()
-    for name in ("u2h", "w0h", "u1h", "w2h", "u3h", "w4h"):
-        plan[name].wait_recv()
-    own_stack = jnp.concatenate([own_head[s] for s in range(4)], axis=0)
-    far_stack = jnp.concatenate([far_head[s] for s in range(4)], axis=0)
-    both_stack = jnp.concatenate([own_stack, far_stack], axis=1)
+
+    arrive("w0h", "w4h")
+    for e in each:
+        arrive(f"u1h{e}")
     part = jnp.zeros((1, LANES), F32)
-    for e in range(local_events):
-        both = jnp.dot(head_matrix(e), both_stack, preferred_element_type=F32)
-        part = part + met(own_field[0, e], both[:, :LANES]) + met(far_field[0, e], both[:, LANES:])
-        one = jnp.dot(head_matrix(local_events + e), own_stack, preferred_element_type=F32)
-        part = part + met(own_field[1, e], one)
-        one = jnp.dot(head_matrix(2 * local_events + e), far_stack, preferred_element_type=F32)
-        part = part + met(far_field[1, e], one)
-    head_sum[0] = part
-    for name in ("head3", "head1", "head2"):
-        plan[name].start()
-
-    for name in ("w0t", "u1t", "w4t"):
-        plan[name].wait_recv()
+    for side, base in ((0, 0), (1, 2 * local_events)):
+        for e in each:
+            part = part + met(far_field[side, e], head_dot(base + e, range(4), far_head))
+    arrive("w0t", "w4t")
     widen(far_tail, 1, far_wide)
     widen(far_tail, 3, far_wide)
-    far_rhs = jnp.concatenate([far_wide[s] for s in range(4)], axis=0)
-    part = jnp.zeros((1, LANES), F32)
-    for g, side in ((0, 0), (2, 1)):
-        for e in range(local_events):
-            k = g * local_events + e
-            one = jnp.dot(tail_matrix(k, range(4)), far_rhs, preferred_element_type=F32)
-            part = part + met(far_bits[side, e], one)
-    tail_sum[0] = part
-    plan["tail"].start()
-
-    plan["u2t"].wait_recv()
-    widen(own_tail, 2, own_wide)
-    own_rhs = jnp.concatenate([own_wide[s] for s in range(3)], axis=0)
+    for e in each:
+        arrive(f"u1t{e}")
+    for side, base in ((0, 0), (1, 2 * local_events)):
+        for e in each:
+            part = part + met(far_bits[side, e], tail_dot(base + e, range(4), far_wide))
+    side_sum[0] = part
+    start("side")
+
     for k in range(2 * local_events):
-        early[k] = jnp.dot(tail_matrix(k, range(3)), own_rhs, preferred_element_type=F32)
-    plan["u3t"].wait_recv()
-    widen(own_tail, 3, own_wide)
-    plan["w2t"].wait_recv()
+        head_sum[k] = head_dot(k, range(2), own_head)
+    arrive("u2h")
+    for k in range(2 * local_events):
+        head_sum[k] += head_dot(k, (2,), own_head)
+    arrive("u3h")
+    for e in each:
+        arrive(f"w2h{e}")
     part = jnp.zeros((1, LANES), F32)
     for g in range(2):
-        for e in range(local_events):
+        for e in each:
             k = g * local_events + e
-            one = early[k] + jnp.dot(
-                tail_matrix(k, (3,)), own_wide[3], preferred_element_type=F32
-            )
-            part = part + met(own_bits[g, e], one)
-    for name in ("head1", "head2", "head3", "tail"):
-        plan[name].wait_recv()
-    heads = head_sum[0] + head_sum[1] + head_sum[2] + head_sum[3]
-    spot = lax.broadcasted_iota(jnp.int32, (1, LANES), 1)
-    mine = (spot >= me * width) & (spot < (me + 1) * width)
-    answer = part + tail_sum[1] + jnp.where(mine, heads, 0.0)
+            part = part + met(own_field[g, e], head_sum[k] + head_dot(k, (3,), own_head))
+    arrive("u2t")
+    widen(own_tail, 2, own_wide)
+    for k in range(2 * local_events):
+        tail_sum[k] = tail_dot(k, range(3), own_wide)
+    arrive("u3t")
+    widen(own_tail, 3, own_wide)
+    for e in each:
+        arrive(f"w2t{e}")
+    for g in range(2):
+        for e in each:
+            k = g * local_events + e
+            part = part + met(own_bits[g, e], tail_sum[k] + tail_dot(k, (3,), own_wide))
+    arrive("side")
+    answer = part + side_sum[1]
     total = answer[:, :width]
     for k in range(1, per_tile):
         total = total + answer[:, k * width : (k + 1) * width]
@@ -475,42 +505,32 @@
         green_tiles = full + (1 if rest else 0)
         strain_tiles = full * local_events + (local_events // fit if rest else 0)
         events = n * local_events
-        pairs = pair_events.shape[1]
-        left = comps - n
-        square = n == 4 and nt == 2 * LANES and 0 < left and 2 * left == per_tile
+        square = n == 4 and nt == 2 * LANES and full == 1 and 2 * rest == per_tile
         if square:
             steps = square_kernel
+            pairs = pair_events.shape[1]
             half = nt // 2
-            head = (4, nt, LANES)
-            field = (2, local_events, nt, LANES)
-            tail = (4, half, LANES)
-            bits = (2, local_events, half, LANES)
+            copies = 17 + 4 * local_events
             scratch = [
                 pltpu.SMEM((1, pairs), jnp.int32),
                 pltpu.SMEM((1,), jnp.int32),
                 pltpu.VMEM((1, pairs, nt), F32),
-                pltpu.VMEM(head, BF16),
-                pltpu.VMEM(head, BF16),
-                pltpu.VMEM(field, BF16),
-                pltpu.VMEM(field, BF16),
-                pltpu.VMEM((left, nt, vox), BF16),
-                pltpu.VMEM((local_events, left, nt, vox), BF16),
-                pltpu.VMEM((2, half, LANES), BF16),
-                pltpu.VMEM(tail, BF16),
-                pltpu.VMEM(tail, BF16),
-                pltpu.VMEM(bits, BF16),
-                pltpu.VMEM(bits, BF16),
-                pltpu.VMEM(bits, BF16),
-                pltpu.VMEM((4, events, nt), F32),
+                pltpu.VMEM((comps, nt, vox), BF16),
+                pltpu.VMEM((local_events, comps, nt, vox), BF16),
+                *(pltpu.VMEM((k, nt, LANES), BF16) for k in (2, 4, 4)),
+                *(pltpu.VMEM((2, local_events, nt, LANES), BF16) for _ in range(3)),
+                *(pltpu.VMEM((k, half, LANES), BF16) for k in (2, 4, 4)),
+                *(pltpu.VMEM((2, local_events, half, LANES), BF16) for _ in range(3)),
+                *(pltpu.VMEM((4, nt, LANES), BF16) for _ in range(2)),
+                pltpu.VMEM((4, events, nt), BF16),
+                pltpu.VMEM((events, nt), F32),
                 pltpu.VMEM((3 * local_events, 4, 2, half, half), BF16),
-                pltpu.VMEM(head, BF16),
-                pltpu.VMEM(head, BF16),
+                pltpu.VMEM((2 * local_events, nt, LANES), F32),
                 pltpu.VMEM((2 * local_events, half, LANES), F32),
-                pltpu.VMEM((4, 1, LANES), F32),
                 pltpu.VMEM((2, 1, LANES), F32),
-                pltpu.SemaphoreType.DMA((9,)),
-                pltpu.SemaphoreType.DMA((23,)),
-                pltpu.SemaphoreType.DMA((23,)),
+                pltpu.SemaphoreType.DMA((5,)),
+                pltpu.SemaphoreType.DMA((copies,)),
+                pltpu.SemaphoreType.DMA((copies,)),
             ]
         else:
             steps = functools.partial(kernel, n)

time: 21 us -> 18.2 us (0.87)
  Pallas kernels: 19.7 us -> 16.9 us
    pallas_call x1, Pallas kernels: 19.7 us -> 16.9 us  [body(): pl.pallas_call(steps, out_shape=pltpu.VMEM((width,), F32), in_specs=[pl.B...]
where the time goes in v2:
time: 18.2 us; the launch traced here: 18.1 us
  Pallas kernels  16.9 us (93%)
  between operations  0.66 us (4%)
  local copies, waits for them, and re-layouts  0.51 us (3%)
    pallas_call x1, Pallas kernels, body(): pl.pallas_call(steps, out_shape=pltpu.VMEM((width,), F32), in_specs=[pl.B...  16.9 us
    unnamed x1, local copies, waits for them, and re-layouts  0.51 us

profile of v2, /device:TPU:0, one launch (start us, length us, event | category | flops | bytes accessed | tf_op | source)
XLA Modules:
  0.0 18.1 jit_solution(14447001696754239535)
XLA Ops:
  0.7 16.9 %shard_map.55 = f32[32]{0:T(128)S(1)} custom-call(s32[1,8]{1,0:T(1,128)} %events_hbm.1, s32[1]{0:T(128)S(6)} %copy.8.counts_hbm, f32[1,8,256]{2,1,0:T(8,128)} %resid_hbm.1, bf16[1,6,256,128]{3,2,1,0:T(8,128)(2,1)} %green_hbm.1, bf16[2,6,256,128]{3,2,1,0:T(8,128)(2,1)} %strain_hbm.1), custom_call_target="tpu_custom_call" | custom-call | tf_op jit(solution)/shard_map/pallas_call | solution.py:551
  17.6 0.5 %copy.7 = f32[32]{0:T(128)} copy(f32[32]{0:T(128)S(1)} %shard_map.55) | data formatting | bytes 256

commit v3 on v2

--- a/solution.py
+++ b/solution.py
@@ -221,7 +221,7 @@
     events_ref, counts_ref, resid, green, strain,
     send_head, own_head, far_head, send_field, own_field, far_field,
     send_tail, own_tail, far_tail, send_bits, own_bits, far_bits, own_wide, far_wide,
-    waves, rows_of, toeplitz, head_sum, tail_sum, side_sum, load_sem, send_sem, recv_sem,
+    waves, rows_of, toeplitz, head_sum, tail_sum, far_head_sum, far_tail_sum, side_sum, load_sem, send_sem, recv_sem,
 ):
     me = lax.axis_index("sta")
     x, y = lax.rem(me, 2), me // 2
@@ -296,9 +296,16 @@
             device_id_type=pl.DeviceIdType.MESH,
         )
 
+    core = lax.rem(lax.axis_index("vox"), 2)
+
     def start(*names):
         for name in names:
             plan[name].start()
+
+    def start_on(which, *names):
+        @pl.when(core == which)
+        def _():
+            start(*names)
 
     def arrive(*names):
         for name in names:
@@ -318,27 +325,31 @@
             parts.append(jnp.where(hit, 1.0, 0.0).astype(BF16))
         return jnp.concatenate(parts, axis=0)
 
-    def packed(pieces, matrix):
-        wide = jnp.concatenate(pieces, axis=1)
-        return jnp.dot(wide, matrix, preferred_element_type=F32).astype(BF16)
-
-    def head_of(source, matrix):
-        return packed([source[k] for k in range(per_tile)], matrix)
-
-    def tail_of(source, matrix):
-        return packed(
+    def wide_head(source):
+        return jnp.concatenate([source[k] for k in range(per_tile)], axis=1)
+
+    def wide_tail(source):
+        return jnp.concatenate(
             [source[per_tile + k, h * half : (h + 1) * half] for h in range(2) for k in range(rest)],
-            matrix,
+            axis=1,
         )
+
+    def pack(wides, pickers, *outs):
+        wide = jnp.concatenate(wides, axis=0)
+        both = jnp.dot(wide, pickers, preferred_element_type=F32).astype(BF16)
+        at = 0
+        for left, right in outs:
+            size = left.shape[0]
+            left[...] = both[at : at + size, :LANES]
+            right[...] = both[at : at + size, LANES:]
+            at += size
 
     def make_toeplitz(s):
         rows_of[...] = waves[s].astype(F32)
 
-        @pl.loop(0, 3 * local_events)
-        def _(k):
-            group = k // local_events
-            owner = me + (group % 2) * (first - me) + (group // 2) * (second - me)
-            wave = rows_of[pl.ds(owner * local_events + k - group * local_events, 1), :]
+        for k in range(3 * local_events):
+            owner = (me, first, second)[k // local_events]
+            wave = rows_of[pl.ds(owner * local_events + k % local_events, 1), :]
             before = 0.0
             for b in range(2):
                 piece = jnp.broadcast_to(wave[:, b * LANES : (b + 1) * LANES], (LANES, LANES))
@@ -353,30 +364,33 @@
 
     nothing = jnp.zeros((half, half), BF16)
 
-    def head_dot(k, stations, heads):
-        top = [toeplitz[k, s, b] for s in stations for b in range(2)]
-        bottom = [piece for s in stations for piece in (nothing, toeplitz[k, s, 0])]
-        matrix = jnp.concatenate(
-            [jnp.concatenate(top, axis=1), jnp.concatenate(bottom, axis=1)], axis=0
+    def top(k, stations):
+        return jnp.concatenate([toeplitz[k, s, b] for s in stations for b in range(2)], axis=1)
+
+    def bottom(k, stations):
+        return jnp.concatenate(
+            [piece for s in stations for piece in (nothing, toeplitz[k, s, 0])], axis=1
         )
-        stack = jnp.concatenate([heads[s] for s in stations], axis=0)
-        return jnp.dot(matrix, stack, preferred_element_type=F32)
-
-    def tail_dot(k, stations, wides):
-        matrix = jnp.concatenate([toeplitz[k, s, b] for s in stations for b in range(2)], axis=1)
-        stack = jnp.concatenate([wides[s] for s in stations], axis=0)
-        return jnp.dot(matrix, stack, preferred_element_type=F32)
+
+    def stack(fields, stations):
+        return jnp.concatenate([fields[s] for s in stations], axis=0)
+
+    def head_dot(ks, stations, field):
+        matrix = jnp.concatenate([f(k, stations) for k in ks for f in (top, bottom)], axis=0)
+        return jnp.dot(matrix, field, preferred_element_type=F32)
+
+    def tail_dot(ks, stations, field):
+        matrix = jnp.concatenate([top(k, stations) for k in ks], axis=0)
+        return jnp.dot(matrix, field, preferred_element_type=F32)
 
     def met(field, adjoint):
         return jnp.sum(field.astype(F32) * adjoint, axis=0, keepdims=True)
 
-    to_across, to_second = picker(across), picker(second)
+    away = jnp.concatenate([picker(across), picker(second)], axis=1)
     loads["green"].wait()
-    send_head[0] = head_of(green, to_across)
+    pack([wide_head(green)], away, (send_head.at[0], send_head.at[1]))
     pl.semaphore_wait(barrier, 2)
-    start("u0h")
-    send_head[1] = head_of(green, to_second)
-    start("w1h")
+    start("u0h", "w1h")
 
     for name in ("events", "counts", "resid"):
         loads[name].wait()
@@ -388,99 +402,109 @@
     waves[0] = comb.astype(BF16)
     start("wave1", "wave2")
 
-    send_tail[0] = tail_of(green, to_across)
-    send_tail[1] = tail_of(green, to_second)
+    pack([wide_tail(green)], away, (send_tail.at[0], send_tail.at[1]))
     start("u0t", "w1t")
-    to_me, to_first = picker(me), picker(first)
-    own_head[0] = head_of(green, to_me)
+    near = jnp.concatenate([picker(me), picker(first)], axis=1)
+    pack(
+        [wide_head(green), wide_tail(green)],
+        near,
+        (own_head.at[0], far_head.at[0]),
+        (own_tail.at[0], far_tail.at[0]),
+    )
+    start("w0h", "w0t")
     loads["strain"].wait()
-    send_field[0, 0] = head_of(strain.at[0], to_across)
-    start("w0h", "u1h0")
+    pack(
+        [f(strain.at[e]) for f in (wide_head, wide_tail) for e in each],
+        away,
+        *((send_field.at[0, e], send_field.at[1, e]) for e in each),
+        *((send_bits.at[0, e], send_bits.at[1, e]) for e in each),
+    )
+    start("u1h0", "u1h1")
     arrive("wave1", "wave2")
-    start("wave3", "wave4")
-    for e in each[1:]:
-        send_field[0, e] = head_of(strain.at[e], to_across)
-        start(f"u1h{e}")
-    own_tail[0] = tail_of(green, to_me)
-    for e in each:
-        send_bits[0, e] = tail_of(strain.at[e], to_across)
+    start("wave3", "wave4", "u1t0", "u1t1")
     arrive("w1h")
-    start("w4h", "w0t")
-    for e in each:
-        start(f"u1t{e}")
+    start("w4h")
     arrive("w1t")
     start("w4t")
-    far_head[0] = head_of(green, to_first)
-    start("u2h")
-    for e in each:
-        send_field[1, e] = head_of(strain.at[e], to_second)
-        start(f"w2h{e}")
+    start_on(0, "u2h", "w2h0", "w2h1")
     arrive("u0h")
-    start("u3h")
-    far_tail[0] = tail_of(green, to_first)
-    for e in each:
-        send_bits[1, e] = tail_of(strain.at[e], to_second)
-        start(f"w2t{e}")
+    start_on(0, "u3h", "u2t", "w2t0", "w2t1")
+    arrive("u0t")
+    start_on(0, "u3t")
+    pack(
+        [f(strain.at[e]) for f in (wide_head, wide_tail) for e in each],
+        near,
+        *((own_field.at[0, e], far_field.at[0, e]) for e in each),
+        *((own_bits.at[0, e], far_bits.at[0, e]) for e in each),
+    )
+    early, late = range(2), (3,)
+    ours = range(2 * local_events)
+    theirs = [*each, *range(2 * local_events, 3 * local_events)]
+
+    def gather(ks, stations, heads, wides, heads_to, tails_to, fresh):
+        field = jnp.concatenate([stack(heads, stations), stack(wides, stations)], axis=1)
+        both = head_dot(ks, stations, field)
+        for i in ours:
+            head, tail = both[i * nt : (i + 1) * nt, :LANES], both[i * nt : i * nt + half, LANES:]
+            heads_to[i] = head if fresh else heads_to[i] + head
+            tails_to[i] = tail if fresh else tails_to[i] + tail
+
     make_toeplitz(0)
+    make_toeplitz(2)
+    widen(far_tail, 0, far_wide)
+    widen(far_tail, 2, far_wide)
+    gather(theirs, (0, 2), far_head, far_wide, far_head_sum, far_tail_sum, True)
     make_toeplitz(1)
-    make_toeplitz(2)
-    for e in each:
-        far_field[0, e] = head_of(strain.at[e], to_first)
-        far_bits[0, e] = tail_of(strain.at[e], to_first)
-        own_field[0, e] = head_of(strain.at[e], to_me)
-        own_bits[0, e] = tail_of(strain.at[e], to_me)
     widen(own_tail, 0, own_wide)
     widen(own_tail, 1, own_wide)
-    widen(far_tail, 0, far_wide)
-    arrive("u0t")
-    widen(far_tail, 2, far_wide)
+    gather(ours, early, own_head, own_wide, head_sum, tail_sum, True)
     arrive("wave3", "wave4")
-    start("u2t", "u3t")
     make_toeplitz(3)
-
-    arrive("w0h", "w4h")
+    arrive("w0h", "w0t")
+    start_on(1, "w2h0", "u2h")
+    widen(far_tail, 1, far_wide)
+    gather(theirs, (1,), far_head, far_wide, far_head_sum, far_tail_sum, False)
+    arrive("w4h", "w4t")
+    start_on(1, "w2h1", "u3h", "u2t", "w2t0", "w2t1", "u3t")
+    widen(far_tail, 3, far_wide)
+    field = jnp.concatenate([far_head[3], far_wide[3]], axis=1)
+    both = head_dot(theirs, late, field)
     for e in each:
-        arrive(f"u1h{e}")
+        arrive(f"u1h{e}", f"u1t{e}")
     part = jnp.zeros((1, LANES), F32)
-    for side, base in ((0, 0), (1, 2 * local_events)):
-        for e in each:
-            part = part + met(far_field[side, e], head_dot(base + e, range(4), far_head))
-    arrive("w0t", "w4t")
-    widen(far_tail, 1, far_wide)
-    widen(far_tail, 3, far_wide)
-    for e in each:
-        arrive(f"u1t{e}")
-    for side, base in ((0, 0), (1, 2 * local_events)):
-        for e in each:
-            part = part + met(far_bits[side, e], tail_dot(base + e, range(4), far_wide))
+    for i in ours:
+        side, e = i // local_events, i % local_events
+        head, tail = both[i * nt : (i + 1) * nt, :LANES], both[i * nt : i * nt + half, LANES:]
+        part = part + met(far_field[side, e], far_head_sum[i] + head)
+        part = part + met(far_bits[side, e], far_tail_sum[i] + tail)
     side_sum[0] = part
     start("side")
 
-    for k in range(2 * local_events):
-        head_sum[k] = head_dot(k, range(2), own_head)
     arrive("u2h")
-    for k in range(2 * local_events):
-        head_sum[k] += head_dot(k, (2,), own_head)
+    two = head_dot(ours, (2,), own_head[2])
+    for k in ours:
+        head_sum[k] += two[k * nt : (k + 1) * nt]
     arrive("u3h")
+    three = head_dot(ours, late, own_head[3])
     for e in each:
         arrive(f"w2h{e}")
     part = jnp.zeros((1, LANES), F32)
-    for g in range(2):
-        for e in each:
-            k = g * local_events + e
-            part = part + met(own_field[g, e], head_sum[k] + head_dot(k, (3,), own_head))
+    for k in ours:
+        field = own_field[k // local_events, k % local_events]
+        part = part + met(field, head_sum[k] + three[k * nt : (k + 1) * nt])
     arrive("u2t")
     widen(own_tail, 2, own_wide)
-    for k in range(2 * local_events):
-        tail_sum[k] = tail_dot(k, range(3), own_wide)
+    two = tail_dot(ours, (2,), own_wide[2])
+    for k in ours:
+        tail_sum[k] += two[k * half : (k + 1) * half]
     arrive("u3t")
     widen(own_tail, 3, own_wide)
+    three = tail_dot(ours, late, own_wide[3])
     for e in each:
         arrive(f"w2t{e}")
-    for g in range(2):
-        for e in each:
-            k = g * local_events + e
-            part = part + met(own_bits[g, e], tail_sum[k] + tail_dot(k, (3,), own_wide))
+    for k in ours:
+        field = own_bits[k // local_events, k % local_events]
+        part = part + met(field, tail_sum[k] + three[k * half : (k + 1) * half])
     arrive("side")
     answer = part + side_sum[1]
     total = answer[:, :width]
@@ -525,6 +549,8 @@
                 pltpu.VMEM((4, events, nt), BF16),
                 pltpu.VMEM((events, nt), F32),
                 pltpu.VMEM((3 * local_events, 4, 2, half, half), BF16),
+                pltpu.VMEM((2 * local_events, nt, LANES), F32),
+                pltpu.VMEM((2 * local_events, half, LANES), F32),
                 pltpu.VMEM((2 * local_events, nt, LANES), F32),
                 pltpu.VMEM((2 * local_events, half, LANES), F32),
                 pltpu.VMEM((2, 1, LANES), F32),

time: 18.2 us -> 17.6 us (0.967)
  Pallas kernels: 16.9 us -> 16.3 us
    pallas_call x1, Pallas kernels: 16.9 us -> 16.3 us  [body(): pl.pallas_call(steps, out_shape=pltpu.VMEM((width,), F32), in_specs=[pl.B...]
where the time goes in v3:
time: 17.6 us; the launch traced here: 17.4 us
  Pallas kernels  16.3 us (93%)
  between operations  0.66 us (4%)
  local copies, waits for them, and re-layouts  0.51 us (3%)
    pallas_call x1, Pallas kernels, body(): pl.pallas_call(steps, out_shape=pltpu.VMEM((width,), F32), in_specs=[pl.B...  16.3 us
    unnamed x1, local copies, waits for them, and re-layouts  0.51 us

profile of v3, /device:TPU:0, one launch (start us, length us, event | category | flops | bytes accessed | tf_op | source)
XLA Modules:
  0.0 17.4 jit_solution(3744523898512861263)
XLA Ops:
  0.7 16.3 %shard_map.55 = f32[32]{0:T(128)S(1)} custom-call(s32[1,8]{1,0:T(1,128)} %events_hbm.1, s32[1]{0:T(128)S(6)} %copy.8.counts_hbm, f32[1,8,256]{2,1,0:T(8,128)} %resid_hbm.1, bf16[1,6,256,128]{3,2,1,0:T(8,128)(2,1)} %green_hbm.1, bf16[2,6,256,128]{3,2,1,0:T(8,128)(2,1)} %strain_hbm.1), custom_call_target="tpu_custom_call" | custom-call | tf_op jit(solution)/shard_map/pallas_call | solution.py:577
  16.9 0.5 %copy.7 = f32[32]{0:T(128)} copy(f32[32]{0:T(128)S(1)} %shard_map.55) | data formatting | bytes 256

commit v4 on v3

--- a/solution.py
+++ b/solution.py
@@ -461,11 +461,10 @@
     arrive("wave3", "wave4")
     make_toeplitz(3)
     arrive("w0h", "w0t")
-    start_on(1, "w2h0", "u2h")
     widen(far_tail, 1, far_wide)
     gather(theirs, (1,), far_head, far_wide, far_head_sum, far_tail_sum, False)
+    start_on(1, "w2h0", "w2h1", "u2h", "u3h", "u2t", "w2t0", "w2t1", "u3t")
     arrive("w4h", "w4t")
-    start_on(1, "w2h1", "u3h", "u2t", "w2t0", "w2t1", "u3t")
     widen(far_tail, 3, far_wide)
     field = jnp.concatenate([far_head[3], far_wide[3]], axis=1)
     both = head_dot(theirs, late, field)

time: 17.6 us -> 17.6 us (level)
  no operation moved by 1% of the time
where the time goes in v4:
time: 17.6 us; the launch traced here: 17.5 us
  Pallas kernels  16.3 us (93%)
  between operations  0.66 us (4%)
  local copies, waits for them, and re-layouts  0.51 us (3%)
    pallas_call x1, Pallas kernels, body(): pl.pallas_call(steps, out_shape=pltpu.VMEM((width,), F32), in_specs=[pl.B...  16.3 us
    unnamed x1, local copies, waits for them, and re-layouts  0.51 us

profile of v4, /device:TPU:0, one launch (start us, length us, event | category | flops | bytes accessed | tf_op | source)
XLA Modules:
  0.0 17.5 jit_solution(2969930701304258282)
XLA Ops:
  0.7 16.3 %shard_map.55 = f32[32]{0:T(128)S(1)} custom-call(s32[1,8]{1,0:T(1,128)} %events_hbm.1, s32[1]{0:T(128)S(6)} %copy.8.counts_hbm, f32[1,8,256]{2,1,0:T(8,128)} %resid_hbm.1, bf16[1,6,256,128]{3,2,1,0:T(8,128)(2,1)} %green_hbm.1, bf16[2,6,256,128]{3,2,1,0:T(8,128)(2,1)} %strain_hbm.1), custom_call_target="tpu_custom_call" | custom-call | tf_op jit(solution)/shard_map/pallas_call | solution.py:576
  16.9 0.5 %copy.7 = f32[32]{0:T(128)} copy(f32[32]{0:T(128)S(1)} %shard_map.55) | data formatting | bytes 256

commit v5 on v4

--- a/solution.py
+++ b/solution.py
@@ -411,7 +411,7 @@
         (own_head.at[0], far_head.at[0]),
         (own_tail.at[0], far_tail.at[0]),
     )
-    start("w0h", "w0t")
+    start("w0h")
     loads["strain"].wait()
     pack(
         [f(strain.at[e]) for f in (wide_head, wide_tail) for e in each],
@@ -420,10 +420,10 @@
         *((send_bits.at[0, e], send_bits.at[1, e]) for e in each),
     )
     start("u1h0", "u1h1")
+    arrive("w1h")
+    start("w4h", "w0t")
     arrive("wave1", "wave2")
     start("wave3", "wave4", "u1t0", "u1t1")
-    arrive("w1h")
-    start("w4h")
     arrive("w1t")
     start("w4t")
     start_on(0, "u2h", "w2h0", "w2h1")

time: 17.6 us -> 17.5 us (level)
  Pallas kernels: 16.3 us -> 16.1 us
where the time goes in v5:
time: 17.5 us; the launch traced here: 17.3 us
  Pallas kernels  16.1 us (92%)
  between operations  0.66 us (4%)
  local copies, waits for them, and re-layouts  0.51 us (3%)
    pallas_call x1, Pallas kernels, body(): pl.pallas_call(steps, out_shape=pltpu.VMEM((width,), F32), in_specs=[pl.B...  16.1 us
    unnamed x1, local copies, waits for them, and re-layouts  0.51 us

profile of v5, /device:TPU:0, one launch (start us, length us, event | category | flops | bytes accessed | tf_op | source)
XLA Modules:
  0.0 17.3 jit_solution(8140600645923934723)
XLA Ops:
  0.7 16.1 %shard_map.55 = f32[32]{0:T(128)S(1)} custom-call(s32[1,8]{1,0:T(1,128)} %events_hbm.1, s32[1]{0:T(128)S(6)} %copy.8.counts_hbm, f32[1,8,256]{2,1,0:T(8,128)} %resid_hbm.1, bf16[1,6,256,128]{3,2,1,0:T(8,128)(2,1)} %green_hbm.1, bf16[2,6,256,128]{3,2,1,0:T(8,128)(2,1)} %strain_hbm.1), custom_call_target="tpu_custom_call" | custom-call | tf_op jit(solution)/shard_map/pallas_call | solution.py:576
  16.8 0.5 %copy.7 = f32[32]{0:T(128)} copy(f32[32]{0:T(128)S(1)} %shard_map.55) | data formatting | bytes 256
